TPU v7x, 512 devices: a 8x2x16 block of a 8x8x16 slice. The times are simulated.
512 devices in a mesh: job: 2 (over y), row: 16 (over z), col: 8 (over x), samp: 2 (over core).
Axes of the slice: x: 8, y: 2, z: 16, core: 2. Of those that a mesh axis runs over, the one named last changes fastest.
The devices are a block of a 8x8x16 slice.
Arguments:
- pair_repr: bfloat16 [1024, 512, 128], P(('job', 'row'), ('col', 'samp')), parts along dimension 0, may hold values from -100 to 100
- asym_id: int32 [1024], P('job'), parts along dimension 0, may hold values from 0 to 7, never falling along the last dimension, each value on 1 to 128 neighbouring positions
- valid_len: int32 [2], P('job'), parts along dimension 0, may hold values from 256 to 512
- rel_embed: bfloat16 [128, 128], replicated, may hold values from -12 to 12
- pair_gain: float32 [128], replicated, may hold values from 0.25 to 1.75
- bias_weight: bfloat16 [128, 16], replicated, may hold values from -64 to 64
- tokens: bfloat16 [128, 512, 768], P(('job', 'col', 'samp'), 'row'), parts along dimension 0, may hold values from -6 to 6
- token_gain: float32 [1, 768], replicated, may hold values from 0.25 to 1.75
- qkv_weight: bfloat16 [1, 3, 768, 768], P(None, None, None, 'row'), may hold values from -0.21875 to 0.21875
- out_weight: bfloat16 [1, 768, 768], P(None, 'row'), may hold values from -0.21875 to 0.21875
Outputs:
- refined: bfloat16 [128, 512, 768], P(('job', 'col', 'samp'), 'row'), parts along dimension 0
There are 2 independent parts, one for each index of `job`. A program takes and returns all parts, laid end to end along the dimension named above; an argument that names none is the same for every part. Nothing has to cross between parts.
Inputs may be any that keep to these rules, and one draw needn't show every extreme that they name: `asym_id`: chain indices never fall along the tokens.
All inputs are finite; a program needn't handle non-finite values.
Results may differ from a plain program's by a relative error of at most 0.002.
The roundings to bfloat16 on the way count: a program that leaves them out, or rounds other values in their place, can miss the bound.
Values may be sent and summed in bfloat16 or wider, within the bound.
No kernel may reach another device: no remote copies, remote signals or barrier semaphores. Data moves between devices by JAX's collectives and lax.ppermute only.
A program may use at most 64 MiB of HBM per device.

v0:
```python
import math
import jax
import jax.numpy as jnp
from jax import lax
from jax.sharding import PartitionSpec as P

HEAD_DIM = 48
epsilon = 1e-05


def joined_along(tiles, dim):
    dims = list(tiles.shape[1:])
    dims[dim] *= tiles.shape[0]
    return jnp.moveaxis(tiles, 0, dim).reshape(dims)


def from_everyone(shard, axis):
    copies = jnp.broadcast_to(shard, (lax.axis_size(axis), *shard.shape))
    return lax.all_to_all(copies, axis, split_axis=0, concat_axis=0, tiled=True)


def gathered_copies(shard, axis, dim):
    return joined_along(from_everyone(shard, axis), dim)


def normalize(values, gain_vector):
    average = jnp.mean(values, axis=-1, keepdims=True)
    centered = values - average
    variance = jnp.mean(centered * centered, axis=-1, keepdims=True)
    return centered * lax.rsqrt(variance + epsilon) * gain_vector


def bias_tile_of(pair_repr, asym_id, rel_embed, pair_gain, bias_weight):
    tile_rows, tile_cols, channels = pair_repr.shape
    bin_count = rel_embed.shape[0]
    reach_max = bin_count // 2 - 1
    first_row = lax.axis_index("row") * tile_rows
    first_col = lax.axis_index(("col", "samp")) * tile_cols
    row_ids = first_row + jnp.arange(tile_rows, dtype=jnp.int32)
    col_ids = first_col + jnp.arange(tile_cols, dtype=jnp.int32)
    row_chain = lax.dynamic_slice_in_dim(asym_id, first_row, tile_rows, 0)
    col_chain = lax.dynamic_slice_in_dim(asym_id, first_col, tile_cols, 0)
    offset = jnp.clip(row_ids[:, None] - col_ids[None, :], -reach_max, reach_max) + reach_max
    bin_ids = jnp.where(row_chain[:, None] == col_chain[None, :], offset, bin_count - 1)
    onehot = (
        bin_ids.reshape(-1)[:, None] == jnp.arange(bin_count, dtype=jnp.int32)[None, :]
    ).astype(jnp.bfloat16)
    summed = pair_repr.reshape(-1, channels).astype(jnp.float32) + jnp.dot(
        onehot, rel_embed, preferred_element_type=jnp.float32
    )
    normed = normalize(summed, pair_gain).astype(jnp.bfloat16)
    projected = lax.dot_general(
        bias_weight, normed, (((0,), (1,)), ((), ())), preferred_element_type=jnp.float32
    )
    return projected.reshape(bias_weight.shape[1], tile_rows, tile_cols)


def attend(queries, key_rows, value_rows, pair_bias, keymask, score_scale):
    head_count, query_count, key_count = pair_bias.shape
    model_width = queries.shape[-1]
    head_width = model_width // head_count
    query_h = queries.reshape(query_count, head_count, head_width)
    key_h = key_rows.reshape(key_count, head_count, head_width)
    value_h = value_rows.reshape(key_count, head_count, head_width)
    scores = (
        jnp.einsum("ihd,jhd->hij", query_h, key_h, preferred_element_type=jnp.float32) * score_scale
        + pair_bias
    )
    scores = jnp.where(keymask[None, None, :], scores, -1e30)
    row_max = jnp.max(scores, axis=-1, keepdims=True)
    weights = jnp.where(keymask[None, None, :], jnp.exp(scores - row_max), 0.0)
    row_total = jnp.sum(weights, axis=-1, keepdims=True)
    probs = (weights / row_total).astype(jnp.bfloat16)
    attended = jnp.einsum("hij,jhd->ihd", probs, value_h, preferred_element_type=jnp.float32)
    return attended.reshape(query_count, model_width).astype(jnp.bfloat16)


def per_device(
    pair_repr,
    asym_id,
    valid_len,
    rel_embed,
    pair_gain,
    bias_weight,
    tokens,
    token_gain,
    qkv_weight,
    out_weight,
):
    sample_count, token_rows, model_width = tokens.shape
    total_tokens = asym_id.shape[0]
    keymask = jnp.arange(total_tokens, dtype=jnp.int32) < valid_len[0]
    score_scale = 1.0 / math.sqrt(HEAD_DIM)
    bias_tile = bias_tile_of(pair_repr, asym_id, rel_embed, pair_gain, bias_weight)
    head_tile = lax.all_to_all(bias_tile, "row", split_axis=0, concat_axis=1, tiled=True)
    pair_bias = gathered_copies(head_tile, ("col", "samp"), 2)

    def one_sample(sample_item):
        return attend(
            sample_item[0], sample_item[1], sample_item[2], pair_bias, keymask, score_scale
        )

    current = tokens
    normed = normalize(current.astype(jnp.float32), token_gain[0]).astype(jnp.bfloat16)
    layer_weight = qkv_weight[0]
    projected = jnp.einsum(
        "snc,pcw->psnw",
        lax.all_gather(normed, "row", axis=1, tiled=True),
        layer_weight,
        preferred_element_type=jnp.float32,
    ).astype(jnp.bfloat16)
    head_out = lax.map(one_sample, (projected[0], projected[1], projected[2]))
    attended = lax.all_to_all(head_out, "row", split_axis=1, concat_axis=2, tiled=True)
    flattened = attended.reshape(sample_count * token_rows, model_width)
    update = jnp.dot(
        flattened, gathered_copies(out_weight[0], "row", 0), preferred_element_type=jnp.float32
    )
    current = (
        current.astype(jnp.float32) + update.reshape(sample_count, token_rows, model_width)
    ).astype(jnp.bfloat16)
    return current


def solution(mesh):
    return jax.shard_map(
        per_device,
        mesh=mesh,
        in_specs=(
            P(("job", "row"), ("col", "samp"), None),
            P("job"),
            P("job"),
            P(),
            P(),
            P(),
            P(("job", "col", "samp"), "row", None),
            P(),
            P(None, None, None, "row"),
            P(None, "row", None),
        ),
        out_specs=P(("job", "col", "samp"), "row", None),
        check_vma=False,
    )
```

profile of v0, /device:TPU:66, one launch (start us, length us, event | category | flops | bytes accessed | tf_op | source)
XLA Modules:
  0.0 212.2 jit_solution(4686499185839951413)
XLA Ops:
  6.6 1.1 convert_reduce_fusion
  7.7 1.1 fusion.31
  8.8 0.7 reduce.4
  9.5 1.8 fusion.33
  11.4 0.8 fusion.40
  12.7 1.0 fusion.41
  14.2 56.2 %all_to_all.37 = f32[16,1,1024]{2,1,0:T(1,128)S(1)} all-to-all(f32[16,1,1024]{2,1,0:T(1,128)S(1)} %reshape.165), channel_id=1, replica_groups=mesh['job'=2,'row'=16,'col'=8,'samp'=2] {'row'}, dimensions={0} | all-to-all | bytes 131072 | tf_op jit(solution)/shard_map/all_to_all | solution.py:95
  70.9 0.7 reduce.5
  71.8 1.1 broadcast_in_dim.49
  72.9 7.7 %all-to-all-start.1 = ((f32[16,1,512,32]{2,3,1,0:T(8,128)}), f32[16,1,512,32]{2,3,1,0:T(8,128)S(1)}, u32[]{:S(2)}, u32[]{:S(2)}) async-start(f32[16,1,512,32]{2,3,1,0:T(8,128)} %broadcast_in_dim.49), calls=%async_computation.1 | async-start | bytes 2097152 | tf_op jit(solution)/shard_map/all_to_all | solution.py:19
  80.7 42.3 %all-gather.2.cloned.1.call-done = bf16[4,512,768]{2,1,0:T(8,128)(2,1)} async-done(((bf16[4,32,768]{2,1,0:T(8,128)(2,1)}), bf16[4,512,768]{2,1,0:T(8,128)(2,1)}) %all-gather.2.cloned.1.call-update) | async-done | bytes 3145744 | tf_op jit(solution)/shard_map/all_gather | solution.py:108
  122.9 3.0 %fusion.21 = bf16[3,4,512,48]{2,3,0,1:T(8,128)(2,1)S(1)} fusion(bf16[4,512,768]{2,1,0:T(8,128)(2,1)} %all-gather.2.cloned.1.call-done, bf16[1,3,768,48]{2,3,1,0:T(8,128)(2,1)S(1)} %copy-done), kind=kOutput, calls=%fused_computation.23 | convolution fusion | flops 453279744 | bytes 3956736 | tf_op jit(solution)/shard_map/snc,pcw->psnw/dot_general | solution.py:106
  126.1 6.6 %while.11 = (s32[]{:T(128)}, bf16[4,512,48]{1,2,0:T(8,128)(2,1)S(1)}, bf16[4,512,48]{1,2,0:T(8,128)(2,1)S(1)}, bf16[4,512,48]{1,2,0:T(8,128)(2,1)S(1)}, bf16[4,5...) while((s32[]{:T(128)}, bf16[4,512,48]{1,2,0:T(8,128)(2,1)S(1)}, ...), condition=%wide.region_7.8_spmd.clone, body=%wide.region_4.7_spmd.clone.sunk | while | flops 53239296 | bytes 4405345 | solution.py:112
  126.1 0.7 iota_compare_fusion.4
  127.7 0.7 iota_compare_fusion.4
  129.4 0.7 iota_compare_fusion.4
  131.0 0.7 iota_compare_fusion.4
  133.0 0.8 reshape.167
  133.8 21.0 %all_to_all.38 = bf16[16,2,3072]{2,1,0:T(2,128)(2,1)S(1)} all-to-all(bf16[16,2,3072]{2,1,0:T(2,128)(2,1)S(1)} %reshape.167), channel_id=1, replica_groups=mesh['job'=2,'row'=16,'col'=8,'samp'=2] {'row'}, dimensions={0} | all-to-all | bytes 393216 | tf_op jit(solution)/shard_map/all_to_all | solution.py:113
  154.7 1.1 broadcast_in_dim.50
  155.8 5.2 %all-to-all-start.3 = ((bf16[16,48,768]{2,1,0:T(8,128)(2,1)}), bf16[16,48,768]{2,1,0:T(8,128)(2,1)S(1)}, u32[]{:S(2)}, u32[]{:S(2)}) async-start(bf16[16,48,768]{2,1,0:T(8,128)(2,1)} %broadcast_in_dim.50), calls=%async_computation.3 | async-start | bytes 2359296 | tf_op jit(solution)/shard_map/all_to_all | solution.py:19
  161.0 0.5 reshape.168
  161.7 42.5 %all-to-all-done.3 = bf16[16,48,768]{2,1,0:T(8,128)(2,1)S(1)} async-done(((bf16[16,48,768]{2,1,0:T(8,128)(2,1)}), bf16[16,48,768]{2,1,0:T(8,128)(2,1)S(1)}, u32[]{:S(2)}, u32[]{:S(2)}) %all-to-all-start.3) | async-done | bytes 1179680 | tf_op jit(solution)/shard_map/all_to_all | solution.py:19
  204.2 1.1 fusion.26
  (49 shorter events, 6.1 us)
Async XLA Ops:
  6.5 116.4 %copy-start = (bf16[1,3,768,48]{2,3,1,0:T(8,128)(2,1)S(1)}, bf16[1,3,768,48]{2,3,1,0:T(8,128)(2,1)}, u32[]{:S(2)}) copy-start(bf16[1,3,768,48]{2,3,1,0:T(8,128)(2,1)} %param.20) | copy-start | bytes 663556
  6.6 5.8 %copy-start.2 = (bf16[32,32,128]{2,1,0:T(8,128)(2,1)S(1)}, bf16[32,32,128]{2,1,0:T(8,128)(2,1)}, u32[]{:S(2)}) copy-start(bf16[32,32,128]{2,1,0:T(8,128)(2,1)} %param.12) | copy-start | bytes 786436
  6.6 116.4 %all-gather.2.cloned.1.call-start = ((), (), s32[]{:S(2)}) async-start(), calls=%async_computation.4 | async-start | bytes 3342336 | tf_op jit(solution)/shard_map/all_gather | solution.py:108
  9.5 3.1 %copy-start.4 = (bf16[128,128]{1,0:T(8,128)(2,1)S(1)}, bf16[128,128]{1,0:T(8,128)(2,1)}, u32[]{:S(2)}) copy-start(bf16[128,128]{1,0:T(8,128)(2,1)} %param.15) | copy-start | bytes 98308
  12.4 1.3 copy-start.5
  12.4 1.3 copy-start.6
  72.9 53.1 %all-to-all-start.1 = ((f32[16,1,512,32]{2,3,1,0:T(8,128)}), f32[16,1,512,32]{2,3,1,0:T(8,128)S(1)}, u32[]{:S(2)}, u32[]{:S(2)}) async-start(f32[16,1,512,32]{2,3,1,0:T(8,128)} %broadcast_in_dim.49), calls=%async_computation.1 | async-start | bytes 2097152 | tf_op jit(solution)/shard_map/all_to_all | solution.py:19
  132.6 22.1 %copy-start.3 = (bf16[1,48,768]{2,1,0:T(8,128)(2,1)S(1)}, bf16[1,48,768]{2,1,0:T(8,128)(2,1)}, u32[]{:S(2)}) copy-start(bf16[1,48,768]{2,1,0:T(8,128)(2,1)} %param.21) | copy-start | bytes 221188
  155.8 48.3 %all-to-all-start.3 = ((bf16[16,48,768]{2,1,0:T(8,128)(2,1)}), bf16[16,48,768]{2,1,0:T(8,128)(2,1)S(1)}, u32[]{:S(2)}, u32[]{:S(2)}) async-start(bf16[16,48,768]{2,1,0:T(8,128)(2,1)} %broadcast_in_dim.50), calls=%async_computation.3 | async-start | bytes 2359296 | tf_op jit(solution)/shard_map/all_to_all | solution.py:19
  161.0 43.1 %copy-start.1 = (bf16[4,32,768]{2,1,0:T(8,128)(2,1)S(1)}, bf16[4,32,768]{2,1,0:T(8,128)(2,1)}, u32[]{:S(2)}) copy-start(bf16[4,32,768]{2,1,0:T(8,128)(2,1)} %param.18) | copy-start | bytes 589828
Sparse Core Ops, SparseCore 0:
  11.5 111.4 all-gather.1
where the time goes:
time: 213 us; the launch traced here: 212 us
  waiting for transfers between devices  84.9 us (40%)
  blocking collectives  77.1 us (36%)
  between operations  13.7 us (6%)
  starting transfers between devices  12.9 us (6%)
  other arithmetic  9.07 us (4%)
  matrix products  8.32 us (4%)
  local copies, waits for them, and re-layouts  6.06 us (3%)
    all_to_all x1, blocking collectives, per_device(): lax.all_to_all(bias_tile, 'row', split_axis=0, concat_axis=1, tiled=True)  56.2 us
    all_to_all x2, waiting for transfers between devices, from_everyone(): return lax.all_to_all(copies, axis, split_axis=0, concat_axis=0, tiled=True)  42.5 us
    all_gather x1, waiting for transfers between devices, per_device(): lax.all_gather(normed, 'row', axis=1, tiled=True)  42.3 us
    all_to_all x1, blocking collectives, per_device(): lax.all_to_all(head_out, 'row', split_axis=1, concat_axis=2, tiled=True)  21 us
    all_to_all x2, starting transfers between devices, from_everyone(): return lax.all_to_all(copies, axis, split_axis=0, concat_axis=0, tiled=True)  12.9 us
  transfers between devices with their start and end apart: 3, of which 2 were waited for; matrix products, arithmetic and copies ran while one was open for 4% of the time, Pallas kernels for 0%

commit v1 on v0

--- a/solution.py
+++ b/solution.py
@@ -3,9 +3,13 @@
 import jax.numpy as jnp
 from jax import lax
 from jax.sharding import PartitionSpec as P
+from jax.lax import all_to_all, axis_size
 
 HEAD_DIM = 48
 epsilon = 1e-05
+fill_samples_all = lambda arr_in: jnp.concatenate(
+    all_to_all(jnp.stack([arr_in for _ in range(axis_size("row"))], 0), "row", 0, 0), 1
+)
 
 
 def joined_along(tiles, dim):
@@ -104,10 +108,7 @@
     normed = normalize(current.astype(jnp.float32), token_gain[0]).astype(jnp.bfloat16)
     layer_weight = qkv_weight[0]
     projected = jnp.einsum(
-        "snc,pcw->psnw",
-        lax.all_gather(normed, "row", axis=1, tiled=True),
-        layer_weight,
-        preferred_element_type=jnp.float32,
+        "snc,pcw->psnw", fill_samples_all(normed), layer_weight, preferred_element_type=jnp.float32
     ).astype(jnp.bfloat16)
     head_out = lax.map(one_sample, (projected[0], projected[1], projected[2]))
     attended = lax.all_to_all(head_out, "row", split_axis=1, concat_axis=2, tiled=True)

time: 213 us -> 338 us (1.59)
  the two profiles are of different devices: /device:TPU:66 before, /device:TPU:80 now
where the time goes in v1:
time: 338 us; the launch traced here: 337 us
  waiting for transfers between devices  224 us (66%)
  starting transfers between devices  63.4 us (19%)
  blocking collectives  22.9 us (7%)
  local copies, waits for them, and re-layouts  13.5 us (4%)
  matrix products  6.66 us (2%)
  other arithmetic  6.02 us (2%)
    all_to_all x1, waiting for transfers between devices, all_to_all(jnp.stack([arr_in for _ in range(axis_size('row'))], 0), 'row'...  135 us
    all_to_all x2, waiting for transfers between devices, from_everyone(): return lax.all_to_all(copies, axis, split_axis=0, concat_axis=0, tiled=True)  77.3 us
    all_to_all x1, starting transfers between devices, per_device(): lax.all_to_all(bias_tile, 'row', split_axis=0, concat_axis=1, tiled=True)  43.7 us
    all_to_all x1, blocking collectives, per_device(): lax.all_to_all(head_out, 'row', split_axis=1, concat_axis=2, tiled=True)  22.9 us
    all_to_all x2, starting transfers between devices, from_everyone(): return lax.all_to_all(copies, axis, split_axis=0, concat_axis=0, tiled=True)  15.6 us
    all_to_all x1, waiting for transfers between devices, per_device(): lax.all_to_all(bias_tile, 'row', split_axis=0, concat_axis=1, tiled=True)  12.1 us
  transfers between devices with their start and end apart: 4, of which 4 were waited for; matrix products, arithmetic and copies ran while one was open for 2% of the time, Pallas kernels for 0%

profile of v1, /device:TPU:80, one launch (start us, length us, event | category | flops | bytes accessed | tf_op | source)
XLA Modules:
  0.0 337.2 jit_solution(3251617102425778588)
XLA Ops:
  0.1 1.1 bitcast_convert_fusion
  1.4 0.8 fusion.33
  2.3 1.2 fusion.34
  4.0 0.8 reshape.175
  4.8 43.7 %all-to-all-start.1 = ((f32[16,1,1024]{2,1,0:T(1,128)}), f32[16,1,1024]{2,1,0:T(1,128)S(1)}, u32[]{:S(2)}, u32[]{:S(2)}) async-start(f32[16,1,1024]{2,1,0:T(1,128)} %reshape.175), calls=%async_computation.1 | async-start | bytes 131072 | tf_op jit(solution)/shard_map/all_to_all | solution.py:99
  49.0 12.1 %all-to-all-done.1 = f32[16,1,1024]{2,1,0:T(1,128)S(1)} async-done(((f32[16,1,1024]{2,1,0:T(1,128)}), f32[16,1,1024]{2,1,0:T(1,128)S(1)}, u32[]{:S(2)}, u32[]{:S(2)}) %all-to-all-start.1) | async-done | bytes 65568 | tf_op jit(solution)/shard_map/all_to_all | solution.py:99
  61.2 2.1 stack.2
  63.2 4.2 %all-to-all-start = ((bf16[16,4,32,768]{3,2,1,0:T(8,128)(2,1)}), bf16[16,4,32,768]{3,2,1,0:T(8,128)(2,1)S(1)}, u32[]{:S(2)}, u32[]{:S(2)}) async-start(bf16[16,4,32,768]{3,2,1,0:T(8,128)(2,1)} %stack.2), calls=%async_computation | async-start | bytes 6291456 | tf_op jit(solution)/shard_map/all_to_all | solution.py:11
  67.9 0.8 reduce.5
  68.7 0.8 reshape.176
  69.6 1.0 copy.25
  70.6 134.9 %all-to-all-done = bf16[16,4,32,768]{3,2,1,0:T(8,128)(2,1)S(1)} async-done(((bf16[16,4,32,768]{3,2,1,0:T(8,128)(2,1)}), bf16[16,4,32,768]{3,2,1,0:T(8,128)(2,1)S(1)}, u32[]{:S(2)}, u32[]{:S(2)}) %all-to-all-start) | async-done | bytes 3145760 | tf_op jit(solution)/shard_map/all_to_all | solution.py:11
  205.5 1.2 broadcast_in_dim.49
  207.5 7.6 %all-to-all-start.2 = ((f32[16,1,512,32]{2,3,1,0:T(8,128)}), f32[16,1,512,32]{2,3,1,0:T(8,128)S(1)}, u32[]{:S(2)}, u32[]{:S(2)}) async-start(f32[16,1,512,32]{2,3,1,0:T(8,128)} %broadcast_in_dim.49), calls=%async_computation.2 | async-start | bytes 2097152 | tf_op jit(solution)/shard_map/all_to_all | solution.py:23
  215.1 2.2 copy.23
  217.3 1.2 fusion.16
  218.5 22.9 %all-to-all-done.2 = f32[16,1,512,32]{2,3,1,0:T(8,128)S(1)} async-done(((f32[16,1,512,32]{2,3,1,0:T(8,128)}), f32[16,1,512,32]{2,3,1,0:T(8,128)S(1)}, u32[]{:S(2)}, u32[]{:S(2)}) %all-to-all-start.2) | async-done | bytes 1048608 | tf_op jit(solution)/shard_map/all_to_all | solution.py:23
  241.4 6.6 %while.11 = (s32[]{:T(128)}, bf16[4,512,48]{1,2,0:T(8,128)(2,1)S(1)}, bf16[4,512,48]{1,2,0:T(8,128)(2,1)S(1)}, bf16[4,512,48]{1,2,0:T(8,128)(2,1)S(1)}, bf16[4,5...) while((s32[]{:T(128)}, bf16[4,512,48]{1,2,0:T(8,128)(2,1)S(1)}, ...), condition=%wide.region_7.8_spmd.clone, body=%wide.region_4.7_spmd.clone.sunk | while | flops 53239296 | bytes 4405345 | solution.py:113
  248.3 0.8 reshape.177
  249.1 22.9 %all_to_all.42 = bf16[16,2,3072]{2,1,0:T(2,128)(2,1)S(1)} all-to-all(bf16[16,2,3072]{2,1,0:T(2,128)(2,1)S(1)} %reshape.177), channel_id=1, replica_groups=mesh['job'=2,'row'=16,'col'=8,'samp'=2] {'row'}, dimensions={0} | all-to-all | bytes 393216 | tf_op jit(solution)/shard_map/all_to_all | solution.py:114
  272.0 1.1 broadcast_in_dim.50
  273.1 7.9 %all-to-all-start.4 = ((bf16[16,48,768]{2,1,0:T(8,128)(2,1)}), bf16[16,48,768]{2,1,0:T(8,128)(2,1)S(1)}, u32[]{:S(2)}, u32[]{:S(2)}) async-start(bf16[16,48,768]{2,1,0:T(8,128)(2,1)} %broadcast_in_dim.50), calls=%async_computation.4 | async-start | bytes 2359296 | tf_op jit(solution)/shard_map/all_to_all | solution.py:23
  281.6 54.5 %all-to-all-done.4 = bf16[16,48,768]{2,1,0:T(8,128)(2,1)S(1)} async-done(((bf16[16,48,768]{2,1,0:T(8,128)(2,1)}), bf16[16,48,768]{2,1,0:T(8,128)(2,1)S(1)}, u32[]{:S(2)}, u32[]{:S(2)}) %all-to-all-start.4) | async-done | bytes 1179680 | tf_op jit(solution)/shard_map/all_to_all | solution.py:23
  336.1 1.1 fusion.19
  (53 shorter events, 10.0 us)
Async XLA Ops:
  0.0 217.3 %copy-start = (bf16[1,3,768,48]{2,3,1,0:T(8,128)(2,1)S(1)}, bf16[1,3,768,48]{2,3,1,0:T(8,128)(2,1)}, u32[]{:S(2)}) copy-start(bf16[1,3,768,48]{2,3,1,0:T(8,128)(2,1)} %param.20) | copy-start | bytes 663556
  0.0 3.6 %copy-start.5 = (bf16[128,16]{0,1:T(8,128)(2,1)S(1)}, bf16[128,16]{0,1:T(8,128)(2,1)}, u32[]{:S(2)}) copy-start(bf16[128,16]{0,1:T(8,128)(2,1)} %param.17) | copy-start | bytes 12292
  0.0 3.6 %copy-start.7 = (f32[128]{0:T(128)S(1)}, f32[128]{0:T(128)}, u32[]{:S(2)}) copy-start(f32[128]{0:T(128)} %param.16) | copy-start | bytes 1540
  0.0 48.5 %copy-start.2 = (bf16[4,32,768]{2,1,0:T(8,128)(2,1)S(1)}, bf16[4,32,768]{2,1,0:T(8,128)(2,1)}, u32[]{:S(2)}) copy-start(bf16[4,32,768]{2,1,0:T(8,128)(2,1)} %param.18) | copy-start | bytes 589828
  0.0 48.8 %copy-start.6 = (f32[1,768]{1,0:T(1,128)S(1)}, f32[1,768]{1,0:T(1,128)}, u32[]{:S(2)}) copy-start(f32[1,768]{1,0:T(1,128)} %param.19) | copy-start | bytes 9220
  4.8 56.4 %all-to-all-start.1 = ((f32[16,1,1024]{2,1,0:T(1,128)}), f32[16,1,1024]{2,1,0:T(1,128)S(1)}, u32[]{:S(2)}, u32[]{:S(2)}) async-start(f32[16,1,1024]{2,1,0:T(1,128)} %reshape.175), calls=%async_computation.1 | async-start | bytes 131072 | tf_op jit(solution)/shard_map/all_to_all | solution.py:99
  63.2 142.3 %all-to-all-start = ((bf16[16,4,32,768]{3,2,1,0:T(8,128)(2,1)}), bf16[16,4,32,768]{3,2,1,0:T(8,128)(2,1)S(1)}, u32[]{:S(2)}, u32[]{:S(2)}) async-start(bf16[16,4,32,768]{3,2,1,0:T(8,128)(2,1)} %stack.2), calls=%async_computation | async-start | bytes 6291456 | tf_op jit(solution)/shard_map/all_to_all | solution.py:11
  205.5 2.0 copy-start.1
  207.5 33.9 %all-to-all-start.2 = ((f32[16,1,512,32]{2,3,1,0:T(8,128)}), f32[16,1,512,32]{2,3,1,0:T(8,128)S(1)}, u32[]{:S(2)}, u32[]{:S(2)}) async-start(f32[16,1,512,32]{2,3,1,0:T(8,128)} %broadcast_in_dim.49), calls=%async_computation.2 | async-start | bytes 2097152 | tf_op jit(solution)/shard_map/all_to_all | solution.py:23
  241.4 30.6 %copy-start.4 = (bf16[1,48,768]{2,1,0:T(8,128)(2,1)S(1)}, bf16[1,48,768]{2,1,0:T(8,128)(2,1)}, u32[]{:S(2)}) copy-start(bf16[1,48,768]{2,1,0:T(8,128)(2,1)} %param.21) | copy-start | bytes 221188
  248.3 87.8 %copy-start.3 = (bf16[4,32,768]{2,1,0:T(8,128)(2,1)S(1)}, bf16[4,32,768]{2,1,0:T(8,128)(2,1)}, u32[]{:S(2)}) copy-start(bf16[4,32,768]{2,1,0:T(8,128)(2,1)} %param.18) | copy-start | bytes 589828
  273.1 63.0 %all-to-all-start.4 = ((bf16[16,48,768]{2,1,0:T(8,128)(2,1)}), bf16[16,48,768]{2,1,0:T(8,128)(2,1)S(1)}, u32[]{:S(2)}, u32[]{:S(2)}) async-start(bf16[16,48,768]{2,1,0:T(8,128)(2,1)} %broadcast_in_dim.50), calls=%async_computation.4 | async-start | bytes 2359296 | tf_op jit(solution)/shard_map/all_to_all | solution.py:23
